TPU v7x, 16 devices: a 4x2x1 block of a 4x4x8 slice. The times are simulated.
16 devices in a mesh: dp: 2 (over y, z), fsdp: 8 (over x, core).
Axes of the slice: x: 4, y: 2, z: 1, core: 2. Of those that a mesh axis runs over, the one named last changes fastest.
The devices are a block of a 4x4x8 slice.
Arguments:
- tokens: bfloat16 [256, 128, 2560], P(('dp', 'fsdp')), parts along dimension 0
- gain_in: bfloat16 [2560], P('fsdp')
- w_dq: bfloat16 [2560, 768], P('fsdp')
- gain_q: bfloat16 [768], P('fsdp')
- w_uq: bfloat16 [768, 3840], P('fsdp')
- w_dkv: bfloat16 [2560, 288], P('fsdp')
- gain_kv: bfloat16 [256], P('fsdp')
- w_ukv: bfloat16 [256, 5120], P('fsdp')
- w_out: bfloat16 [2560, 2560], P('fsdp')
Outputs:
- output 1: bfloat16 [256, 128, 2560], P(('dp', 'fsdp')), parts along dimension 0
- output 2: bfloat16 [256, 128, 256], P(('dp', 'fsdp')), parts along dimension 0
- output 3: bfloat16 [256, 128, 32], P(('dp', 'fsdp')), parts along dimension 0
There are 2 independent parts. A program takes and returns all parts, laid end to end along the dimension named above; an argument that names none is the same for every part.
All inputs are finite; a program needn't handle non-finite values.
Results may differ from a plain program's by a relative error of at most 0.00647724.
Values are sent between devices in bfloat16 or wider.
A program may use at most 768 MiB of HBM per device.

v0:
```python
import jax
import jax.numpy as jnp
from jax import lax
from jax.sharding import PartitionSpec as P, NamedSharding

EPSILON = 1e-6
ROPE_THETA = 10000.0


def rms_scale(values_in, gain_vec):
    values_f32 = values_in.astype(jnp.float32)
    inv_rms = lax.rsqrt(jnp.mean(values_f32 * values_f32, axis=-1, keepdims=True) + EPSILON)
    return values_f32 * inv_rms * gain_vec.astype(jnp.float32)


def rope_tables(seq_len, rope_dim):
    half_dim = rope_dim // 2
    inv_freq = ROPE_THETA ** (-2.0 * jnp.arange(half_dim, dtype=jnp.float32) / rope_dim)
    angles = jnp.arange(seq_len, dtype=jnp.float32)[:, None] * inv_freq[None, :]
    return jnp.cos(angles), jnp.sin(angles)


def apply_rope(values_in, cos_t, sin_t):
    half_dim = values_in.shape[-1] // 2
    lo_half = values_in[..., :half_dim]
    hi_half = values_in[..., half_dim:]
    return jnp.concatenate([lo_half * cos_t - hi_half * sin_t, hi_half * cos_t + lo_half * sin_t], axis=-1)


def head_dims(w_uq, w_dkv, gain_kv, w_ukv, w_out):
    rope_dim = w_dkv.shape[1] - gain_kv.shape[0]
    nope_total = w_ukv.shape[1] - w_out.shape[0]
    n_heads = (w_uq.shape[1] - nope_total) // rope_dim
    return n_heads, nope_total // n_heads, rope_dim, w_out.shape[0] // n_heads


def latents(tokens, gain_in, w_dq, gain_q, w_dkv, gain_kv, cos_t, sin_t):
    kv_rank = gain_kv.shape[0]
    normed = rms_scale(tokens, gain_in).astype(jnp.bfloat16)
    q_down = jnp.einsum('btd,dr->btr', normed, w_dq, preferred_element_type=jnp.float32)
    q_lat = rms_scale(q_down, gain_q).astype(jnp.bfloat16)
    kv_down = jnp.einsum('btd,dr->btr', normed, w_dkv, preferred_element_type=jnp.float32)
    latent = rms_scale(kv_down[:, :, :kv_rank], gain_kv).astype(jnp.bfloat16)
    k_pe = apply_rope(kv_down[:, :, kv_rank:], cos_t, sin_t).astype(jnp.bfloat16)
    return q_lat, latent, k_pe


def attend(q_lat, latent, k_pe, w_uq, w_ukv, w_out, head_info, cos_t, sin_t):
    n_heads, nope_dim, rope_dim, v_dim = head_info
    n_prompts = q_lat.shape[0]
    seq_len = q_lat.shape[1]
    q_full = jnp.einsum('btr,rc->btc', q_lat, w_uq, preferred_element_type=jnp.float32)
    q_full = q_full.reshape(n_prompts, seq_len, n_heads, nope_dim + rope_dim)
    q_nope = q_full[..., :nope_dim].astype(jnp.bfloat16)
    q_pe = apply_rope(q_full[..., nope_dim:], cos_t[:, None, :], sin_t[:, None, :]).astype(jnp.bfloat16)
    kv_up = jnp.einsum('btr,rc->btc', latent, w_ukv, preferred_element_type=jnp.float32).astype(jnp.bfloat16)
    kv_up = kv_up.reshape(n_prompts, seq_len, n_heads, nope_dim + v_dim)
    k_nope = kv_up[..., :nope_dim]
    values = kv_up[..., nope_dim:]
    score_scale = (nope_dim + rope_dim) ** -0.5
    scores = jnp.einsum('bqhd,bkhd->bhqk', q_nope, k_nope, preferred_element_type=jnp.float32)
    scores = scores + jnp.einsum('crie,cle->cirl', q_pe, k_pe, preferred_element_type=jnp.float32)
    causal = jnp.arange(seq_len)[:, None] >= jnp.arange(seq_len)[None, :]
    scores = jnp.where(causal, scores * score_scale, -1e30)
    attn_probs = jax.nn.softmax(scores, axis=-1).astype(jnp.bfloat16)
    attn_out = jnp.einsum('bhqk,bkhd->bqhd', attn_probs, values, preferred_element_type=jnp.float32).astype(jnp.bfloat16)
    attn_out = attn_out.reshape(n_prompts, seq_len, n_heads * v_dim)
    return jnp.einsum('btc,cd->btd', attn_out, w_out, preferred_element_type=jnp.float32)


def attend_each(q_lat, latent, k_pe, w_uq, w_ukv, w_out, head_info, cos_t, sin_t):
    def one_prompt(operands):
        q_one, lat_one, pe_one = operands
        return attend(q_one[None], lat_one[None], pe_one[None], w_uq, w_ukv, w_out, head_info, cos_t, sin_t)[0]

    return lax.map(one_prompt, (q_lat, latent, k_pe))


def solution(mesh):
    batch_spec = P(('dp', 'fsdp'))
    row_spec = P('fsdp')
    mat_spec = P('fsdp', None)

    def run_block(tokens, gain_in, w_dq, gain_q, w_uq, w_dkv, gain_kv, w_ukv, w_out):
        head_info = head_dims(w_uq, w_dkv, gain_kv, w_ukv, w_out)
        seq_len = tokens.shape[1]

        def local_block(tok_blk, gain_in_s, w_dq_s, gain_q_s, w_uq_s, w_dkv_s, gain_kv_s, w_ukv_s, w_out_s):
            cos_t, sin_t = rope_tables(seq_len, head_info[2])
            gain_in_all = lax.all_gather(gain_in_s, 'fsdp', tiled=True)
            w_dq_all = lax.all_gather(w_dq_s, 'fsdp', tiled=True)
            gain_q_all = lax.all_gather(gain_q_s, 'fsdp', tiled=True)
            w_dkv_all = lax.all_gather(w_dkv_s, 'fsdp', tiled=True)
            gain_kv_all = lax.all_gather(gain_kv_s, 'fsdp', tiled=True)
            q_lat, latent, k_pe = latents(tok_blk, gain_in_all, w_dq_all, gain_q_all, w_dkv_all, gain_kv_all, cos_t, sin_t)
            w_uq_all = lax.all_gather(w_uq_s, 'fsdp', tiled=True)
            w_ukv_all = lax.all_gather(w_ukv_s, 'fsdp', tiled=True)
            w_out_all = lax.all_gather(w_out_s, 'fsdp', tiled=True)
            proj_out = attend_each(q_lat, latent, k_pe, w_uq_all, w_ukv_all, w_out_all, head_info, cos_t, sin_t)
            y_blk = (tok_blk.astype(jnp.float32) + proj_out).astype(jnp.bfloat16)
            return y_blk, latent, k_pe

        mapped = jax.shard_map(
            local_block,
            mesh=mesh,
            in_specs=(batch_spec, row_spec, mat_spec, row_spec, mat_spec, mat_spec, row_spec, mat_spec, mat_spec),
            out_specs=(batch_spec, batch_spec, batch_spec),
            check_vma=False,
        )
        return mapped(tokens, gain_in, w_dq, gain_q, w_uq, w_dkv, gain_kv, w_ukv, w_out)

    return run_block
```

profile of v0, /device:TPU:113, one launch (start us, length us, event | category | flops | bytes accessed | tf_op | source)
XLA Modules:
  0.0 437.2 jit_solution(2593942455042544608)
XLA Ops:
  14.2 14.1 %all-reduce.3 = (bf16[2560]{0:T(1024)(128)(2,1)S(1)}, bf16[256]{0:T(256)(128)(2,1)S(1)}, bf16[768]{0:T(1024)(128)(2,1)S(1)}) all-reduce(bf16[2560]{0:T(1024)(128)(2,1)S(1)} %dynamic-update-slice, bf16[256]{0:T(256)(128)(2,1)S(1)} %dynamic-update-slice.1, bf16[768]{0:T(1024)(128)(2,1)S(1)} %dynamic-update-slice.2), channel_id=1, replica_groups=mesh['dp'=2,'fsdp'=8] {'fsdp'}, use_global_device_ids=true, to_apply=%add | all-reduce | flops 3584 | bytes 14336
  28.4 6.1 %fusion.29 = f32[16,128]{1,0:T(8,128)S(1)} fusion(bf16[16,128,2560]{2,1,0:T(8,128)(2,1)} %param.11), kind=kLoop, calls=%fused_computation.43 | loop fusion | flops 15726592 | bytes 10493952 | tf_op jit(solution)/shard_map/reduce_sum | solution.py:12
  39.1 6.6 %fusion.35 = f32[16,128,288]{1,2,0:T(8,128)S(1)} fusion(bf16[2560,288,1]{0,1,2:T(8,128)(2,1)} %reshape.199, bf16[16,128,2560]{2,1,0:T(8,128)(2,1)} %param.11, f32[2560]{0:T(1024)S(1)} %convert_element_type.48, f32[16,128]{1,0:T(8,128)S(1)} %add_rsqrt_fusion.2), kind=kOutput, calls=%fused_computation.48 | convolution fusion | flops 3040870400 | bytes 14338048 | tf_op jit(solution)/shard_map/btd,dr->btr/dot_general | solution.py:42
  47.5 14.4 %all-gather.9.cloned.1.call-done = bf16[2560,768]{1,0:T(8,128)(2,1)} async-done(((bf16[320,768]{1,0:T(8,128)(2,1)}), bf16[2560,768]{1,0:T(8,128)(2,1)}) %all-gather.9.cloned.1.call-update) | async-done | bytes 3932176 | tf_op jit(solution)/shard_map/all_gather | solution.py:91
  62.0 12.5 %multiply_reduce_fusion = (f32[16,128]{1,0:T(8,128)S(1)}, f32[16,128,768]{2,1,0:T(8,128)S(1)}) fusion(bf16[2560,768]{1,0:T(8,128)(2,1)} %all-gather.9.cloned.1.call-done, bf16[16,128,2560]{2,1,0:T(8,128)(2,1)} %param.11, f32[2560]{0:T(1024)S(1)} %convert_element_type.48, f32[16,128]{1,0:T(8,128)S(1)} %add_rsqrt_fusion.2), kind=kOutput, calls=%fused_computation.50 | convolution fusion | flops 8077178880 | bytes 20736000 | tf_op jit(solution)/shard_map/btd,dr->btr/dot_general | solution.py:40
  76.7 21.6 %all-gather.11.cloned.1.call-done = bf16[768,3840]{1,0:T(8,128)(2,1)} async-done(((bf16[96,3840]{1,0:T(8,128)(2,1)}), bf16[768,3840]{1,0:T(8,128)(2,1)}) %all-gather.11.cloned.1.call-update) | async-done | bytes 5898256 | tf_op jit(solution)/shard_map/all_gather | solution.py:96
  98.3 8.4 %copy.24 = bf16[768,3840]{0,1:T(8,128)(2,1)} copy(bf16[768,3840]{1,0:T(8,128)(2,1)} %all-gather.11.cloned.1.call-done) | data formatting | bytes 11796480
  106.7 15.1 %all-gather.7.cloned.1.call-done = bf16[256,5120]{1,0:T(8,128)(2,1)} async-done(((bf16[32,5120]{1,0:T(8,128)(2,1)}), bf16[256,5120]{1,0:T(8,128)(2,1)}) %all-gather.7.cloned.1.call-update) | async-done | bytes 2621456 | tf_op jit(solution)/shard_map/all_gather | solution.py:97
  121.9 67.5 %all-gather.13.cloned.1.call-done = bf16[2560,2560]{1,0:T(8,128)(2,1)} async-done(((bf16[320,2560]{1,0:T(8,128)(2,1)}), bf16[2560,2560]{1,0:T(8,128)(2,1)}) %all-gather.13.cloned.1.call-update) | async-done | bytes 13107216 | tf_op jit(solution)/shard_map/all_gather | solution.py:98
  189.4 225.6 %while.13 = (s32[]{:T(128)}, f32[16,128,2560]{2,1,0:T(8,128)}, bf16[16,128,256]{2,1,0:T(8,128)(2,1)}, bf16[256,5120]{1,0:T(8,128)(2,1)}, bf16[16,128,768]{2,1,0:...) while((s32[]{:T(128)}, f32[16,128,2560]{2,1,0:T(8,128)}, ...), condition=%wide.region_6.7_spmd.clone.clone.clone, body=%wide.region_3.6_spmd.clone.clone.clone.sunk | while | flops 2986156032 | bytes 86292232 | solution.py:76
  192.5 4.7 %convolution_bitcast_fusion.3 = f32[1,128,40,96]{1,3,2,0:T(8,128)S(1)} fusion(bf16[40,96,768]{2,1,0:T(8,128)(2,1)} %bitcast.106, bf16[16,128,768]{2,1,0:T(8,128)(2,1)} %get-tuple-element.285, s32[]{:T(128)} %get-tuple-element.271), kind=kOutput, calls=%fused_computation.11.clone.1 | convolution fusion | flops 754974720 | bytes 8061440 | tf_op jit(solution)/shard_map/while/body/eval_jaxpr/btr,rc->btc/dot_general | solution.py:52
  206.6 4.7 %convolution_bitcast_fusion.3 = f32[1,128,40,96]{1,3,2,0:T(8,128)S(1)} fusion(bf16[40,96,768]{2,1,0:T(8,128)(2,1)} %bitcast.106, bf16[16,128,768]{2,1,0:T(8,128)(2,1)} %get-tuple-element.285, s32[]{:T(128)} %get-tuple-element.271), kind=kOutput, calls=%fused_computation.11.clone.1 | convolution fusion | flops 754974720 | bytes 8061440 | tf_op jit(solution)/shard_map/while/body/eval_jaxpr/btr,rc->btc/dot_general | solution.py:52
  220.7 4.7 %convolution_bitcast_fusion.3 = f32[1,128,40,96]{1,3,2,0:T(8,128)S(1)} fusion(bf16[40,96,768]{2,1,0:T(8,128)(2,1)} %bitcast.106, bf16[16,128,768]{2,1,0:T(8,128)(2,1)} %get-tuple-element.285, s32[]{:T(128)} %get-tuple-element.271), kind=kOutput, calls=%fused_computation.11.clone.1 | convolution fusion | flops 754974720 | bytes 8061440 | tf_op jit(solution)/shard_map/while/body/eval_jaxpr/btr,rc->btc/dot_general | solution.py:52
  234.8 4.7 %convolution_bitcast_fusion.3 = f32[1,128,40,96]{1,3,2,0:T(8,128)S(1)} fusion(bf16[40,96,768]{2,1,0:T(8,128)(2,1)} %bitcast.106, bf16[16,128,768]{2,1,0:T(8,128)(2,1)} %get-tuple-element.285, s32[]{:T(128)} %get-tuple-element.271), kind=kOutput, calls=%fused_computation.11.clone.1 | convolution fusion | flops 754974720 | bytes 8061440 | tf_op jit(solution)/shard_map/while/body/eval_jaxpr/btr,rc->btc/dot_general | solution.py:52
  248.8 4.7 %convolution_bitcast_fusion.3 = f32[1,128,40,96]{1,3,2,0:T(8,128)S(1)} fusion(bf16[40,96,768]{2,1,0:T(8,128)(2,1)} %bitcast.106, bf16[16,128,768]{2,1,0:T(8,128)(2,1)} %get-tuple-element.285, s32[]{:T(128)} %get-tuple-element.271), kind=kOutput, calls=%fused_computation.11.clone.1 | convolution fusion | flops 754974720 | bytes 8061440 | tf_op jit(solution)/shard_map/while/body/eval_jaxpr/btr,rc->btc/dot_general | solution.py:52
  262.9 4.7 %convolution_bitcast_fusion.3 = f32[1,128,40,96]{1,3,2,0:T(8,128)S(1)} fusion(bf16[40,96,768]{2,1,0:T(8,128)(2,1)} %bitcast.106, bf16[16,128,768]{2,1,0:T(8,128)(2,1)} %get-tuple-element.285, s32[]{:T(128)} %get-tuple-element.271), kind=kOutput, calls=%fused_computation.11.clone.1 | convolution fusion | flops 754974720 | bytes 8061440 | tf_op jit(solution)/shard_map/while/body/eval_jaxpr/btr,rc->btc/dot_general | solution.py:52
  277.0 4.7 %convolution_bitcast_fusion.3 = f32[1,128,40,96]{1,3,2,0:T(8,128)S(1)} fusion(bf16[40,96,768]{2,1,0:T(8,128)(2,1)} %bitcast.106, bf16[16,128,768]{2,1,0:T(8,128)(2,1)} %get-tuple-element.285, s32[]{:T(128)} %get-tuple-element.271), kind=kOutput, calls=%fused_computation.11.clone.1 | convolution fusion | flops 754974720 | bytes 8061440 | tf_op jit(solution)/shard_map/while/body/eval_jaxpr/btr,rc->btc/dot_general | solution.py:52
  291.2 4.7 %convolution_bitcast_fusion.3 = f32[1,128,40,96]{1,3,2,0:T(8,128)S(1)} fusion(bf16[40,96,768]{2,1,0:T(8,128)(2,1)} %bitcast.106, bf16[16,128,768]{2,1,0:T(8,128)(2,1)} %get-tuple-element.285, s32[]{:T(128)} %get-tuple-element.271), kind=kOutput, calls=%fused_computation.11.clone.1 | convolution fusion | flops 754974720 | bytes 8061440 | tf_op jit(solution)/shard_map/while/body/eval_jaxpr/btr,rc->btc/dot_general | solution.py:52
  319.4 4.7 %convolution_bitcast_fusion.3 = f32[1,128,40,96]{1,3,2,0:T(8,128)S(1)} fusion(bf16[40,96,768]{2,1,0:T(8,128)(2,1)} %bitcast.106, bf16[16,128,768]{2,1,0:T(8,128)(2,1)} %get-tuple-element.285, s32[]{:T(128)} %get-tuple-element.271), kind=kOutput, calls=%fused_computation.11.clone.1 | convolution fusion | flops 754974720 | bytes 8061440 | tf_op jit(solution)/shard_map/while/body/eval_jaxpr/btr,rc->btc/dot_general | solution.py:52
  333.5 4.7 %convolution_bitcast_fusion.3 = f32[1,128,40,96]{1,3,2,0:T(8,128)S(1)} fusion(bf16[40,96,768]{2,1,0:T(8,128)(2,1)} %bitcast.106, bf16[16,128,768]{2,1,0:T(8,128)(2,1)} %get-tuple-element.285, s32[]{:T(128)} %get-tuple-element.271), kind=kOutput, calls=%fused_computation.11.clone.1 | convolution fusion | flops 754974720 | bytes 8061440 | tf_op jit(solution)/shard_map/while/body/eval_jaxpr/btr,rc->btc/dot_general | solution.py:52
  347.6 4.7 %convolution_bitcast_fusion.3 = f32[1,128,40,96]{1,3,2,0:T(8,128)S(1)} fusion(bf16[40,96,768]{2,1,0:T(8,128)(2,1)} %bitcast.106, bf16[16,128,768]{2,1,0:T(8,128)(2,1)} %get-tuple-element.285, s32[]{:T(128)} %get-tuple-element.271), kind=kOutput, calls=%fused_computation.11.clone.1 | convolution fusion | flops 754974720 | bytes 8061440 | tf_op jit(solution)/shard_map/while/body/eval_jaxpr/btr,rc->btc/dot_general | solution.py:52
  389.9 4.7 %convolution_bitcast_fusion.3 = f32[1,128,40,96]{1,3,2,0:T(8,128)S(1)} fusion(bf16[40,96,768]{2,1,0:T(8,128)(2,1)} %bitcast.106, bf16[16,128,768]{2,1,0:T(8,128)(2,1)} %get-tuple-element.285, s32[]{:T(128)} %get-tuple-element.271), kind=kOutput, calls=%fused_computation.11.clone.1 | convolution fusion | flops 754974720 | bytes 8061440 | tf_op jit(solution)/shard_map/while/body/eval_jaxpr/btr,rc->btc/dot_general | solution.py:52
  404.0 4.7 %convolution_bitcast_fusion.3 = f32[1,128,40,96]{1,3,2,0:T(8,128)S(1)} fusion(bf16[40,96,768]{2,1,0:T(8,128)(2,1)} %bitcast.106, bf16[16,128,768]{2,1,0:T(8,128)(2,1)} %get-tuple-element.285, s32[]{:T(128)} %get-tuple-element.271), kind=kOutput, calls=%fused_computation.11.clone.1 | convolution fusion | flops 754974720 | bytes 8061440 | tf_op jit(solution)/shard_map/while/body/eval_jaxpr/btr,rc->btc/dot_general | solution.py:52
  415.0 15.7 %fusion.32 = bf16[16,128,2560]{2,1,0:T(8,128)(2,1)} fusion(f32[16,128,2560]{2,1,0:T(8,128)} %get-tuple-element.61, bf16[16,128,2560]{2,1,0:T(8,128)(2,1)} %param.11), kind=kLoop, calls=%fused_computation.46 | loop fusion | flops 15728640 | bytes 41943040 | tf_op jit(solution)/shard_map/convert_element_type | solution.py:100
  (352 shorter events, 176.9 us)
Async XLA Ops:
  7.2 27.4 %all-gather.15.cloned.1.call-start = ((), (), s32[]{:S(2)}) async-start(), calls=%async_computation.4 | async-start | bytes 1990656 | tf_op jit(solution)/shard_map/all_gather | solution.py:93
  8.0 53.9 %all-gather.9.cloned.1.call-start = ((), (), s32[]{:S(2)}) async-start(), calls=%async_computation.1 | async-start | bytes 4423680 | tf_op jit(solution)/shard_map/all_gather | solution.py:91
  8.8 89.5 %all-gather.11.cloned.1.call-start = ((), (), s32[]{:S(2)}) async-start(), calls=%async_computation.2 | async-start | bytes 6635520 | tf_op jit(solution)/shard_map/all_gather | solution.py:96
  9.6 112.2 %all-gather.7.cloned.1.call-start = ((), (), s32[]{:S(2)}) async-start(), calls=%async_computation | async-start | bytes 2949120 | tf_op jit(solution)/shard_map/all_gather | solution.py:97
  10.3 179.1 %all-gather.13.cloned.1.call-start = ((), (), s32[]{:S(2)}) async-start(), calls=%async_computation.3 | async-start | bytes 14745600 | tf_op jit(solution)/shard_map/all_gather | solution.py:98
  192.4 7.3 %slice-start = ((s8[13107200]{0:T(1024)(128)(4,1)}), s8[4194304]{0:T(1024)(128)(4,1)S(1)}, s32[]{:S(2)}) async-start(s8[13107200]{0:T(1024)(128)(4,1)} %bitcast.104), calls=%async_computation.5 | async-start | bytes 8388608 | tf_op jit(solution)/shard_map/while
  220.6 7.3 %slice-start = ((s8[13107200]{0:T(1024)(128)(4,1)}), s8[4194304]{0:T(1024)(128)(4,1)S(1)}, s32[]{:S(2)}) async-start(s8[13107200]{0:T(1024)(128)(4,1)} %bitcast.104), calls=%async_computation.5 | async-start | bytes 8388608 | tf_op jit(solution)/shard_map/while
  220.6 7.3 %slice-start.1 = ((s8[13107200]{0:T(1024)(128)(4,1)}), s8[4194304]{0:T(1024)(128)(4,1)S(1)}, s32[]{:S(2)}) async-start(s8[13107200]{0:T(1024)(128)(4,1)} %bitcast.104), calls=%async_computation.6 | async-start | bytes 8388608 | tf_op jit(solution)/shard_map/while
  234.7 7.3 %slice-start = ((s8[13107200]{0:T(1024)(128)(4,1)}), s8[4194304]{0:T(1024)(128)(4,1)S(1)}, s32[]{:S(2)}) async-start(s8[13107200]{0:T(1024)(128)(4,1)} %bitcast.104), calls=%async_computation.5 | async-start | bytes 8388608 | tf_op jit(solution)/shard_map/while
  234.7 7.3 %slice-start.1 = ((s8[13107200]{0:T(1024)(128)(4,1)}), s8[4194304]{0:T(1024)(128)(4,1)S(1)}, s32[]{:S(2)}) async-start(s8[13107200]{0:T(1024)(128)(4,1)} %bitcast.104), calls=%async_computation.6 | async-start | bytes 8388608 | tf_op jit(solution)/shard_map/while
  248.8 7.3 %slice-start = ((s8[13107200]{0:T(1024)(128)(4,1)}), s8[4194304]{0:T(1024)(128)(4,1)S(1)}, s32[]{:S(2)}) async-start(s8[13107200]{0:T(1024)(128)(4,1)} %bitcast.104), calls=%async_computation.5 | async-start | bytes 8388608 | tf_op jit(solution)/shard_map/while
  248.8 7.3 %slice-start.1 = ((s8[13107200]{0:T(1024)(128)(4,1)}), s8[4194304]{0:T(1024)(128)(4,1)S(1)}, s32[]{:S(2)}) async-start(s8[13107200]{0:T(1024)(128)(4,1)} %bitcast.104), calls=%async_computation.6 | async-start | bytes 8388608 | tf_op jit(solution)/shard_map/while
  262.9 7.3 %slice-start = ((s8[13107200]{0:T(1024)(128)(4,1)}), s8[4194304]{0:T(1024)(128)(4,1)S(1)}, s32[]{:S(2)}) async-start(s8[13107200]{0:T(1024)(128)(4,1)} %bitcast.104), calls=%async_computation.5 | async-start | bytes 8388608 | tf_op jit(solution)/shard_map/while
  262.9 7.3 %slice-start.1 = ((s8[13107200]{0:T(1024)(128)(4,1)}), s8[4194304]{0:T(1024)(128)(4,1)S(1)}, s32[]{:S(2)}) async-start(s8[13107200]{0:T(1024)(128)(4,1)} %bitcast.104), calls=%async_computation.6 | async-start | bytes 8388608 | tf_op jit(solution)/shard_map/while
  277.0 7.3 %slice-start = ((s8[13107200]{0:T(1024)(128)(4,1)}), s8[4194304]{0:T(1024)(128)(4,1)S(1)}, s32[]{:S(2)}) async-start(s8[13107200]{0:T(1024)(128)(4,1)} %bitcast.104), calls=%async_computation.5 | async-start | bytes 8388608 | tf_op jit(solution)/shard_map/while
  277.0 7.3 %slice-start.1 = ((s8[13107200]{0:T(1024)(128)(4,1)}), s8[4194304]{0:T(1024)(128)(4,1)S(1)}, s32[]{:S(2)}) async-start(s8[13107200]{0:T(1024)(128)(4,1)} %bitcast.104), calls=%async_computation.6 | async-start | bytes 8388608 | tf_op jit(solution)/shard_map/while
  291.2 7.3 %slice-start = ((s8[13107200]{0:T(1024)(128)(4,1)}), s8[4194304]{0:T(1024)(128)(4,1)S(1)}, s32[]{:S(2)}) async-start(s8[13107200]{0:T(1024)(128)(4,1)} %bitcast.104), calls=%async_computation.5 | async-start | bytes 8388608 | tf_op jit(solution)/shard_map/while
  291.2 7.3 %slice-start.1 = ((s8[13107200]{0:T(1024)(128)(4,1)}), s8[4194304]{0:T(1024)(128)(4,1)S(1)}, s32[]{:S(2)}) async-start(s8[13107200]{0:T(1024)(128)(4,1)} %bitcast.104), calls=%async_computation.6 | async-start | bytes 8388608 | tf_op jit(solution)/shard_map/while
  333.5 7.3 %slice-start = ((s8[13107200]{0:T(1024)(128)(4,1)}), s8[4194304]{0:T(1024)(128)(4,1)S(1)}, s32[]{:S(2)}) async-start(s8[13107200]{0:T(1024)(128)(4,1)} %bitcast.104), calls=%async_computation.5 | async-start | bytes 8388608 | tf_op jit(solution)/shard_map/while
  333.5 7.3 %slice-start.1 = ((s8[13107200]{0:T(1024)(128)(4,1)}), s8[4194304]{0:T(1024)(128)(4,1)S(1)}, s32[]{:S(2)}) async-start(s8[13107200]{0:T(1024)(128)(4,1)} %bitcast.104), calls=%async_computation.6 | async-start | bytes 8388608 | tf_op jit(solution)/shard_map/while
  347.6 7.3 %slice-start = ((s8[13107200]{0:T(1024)(128)(4,1)}), s8[4194304]{0:T(1024)(128)(4,1)S(1)}, s32[]{:S(2)}) async-start(s8[13107200]{0:T(1024)(128)(4,1)} %bitcast.104), calls=%async_computation.5 | async-start | bytes 8388608 | tf_op jit(solution)/shard_map/while
  403.9 7.3 %slice-start = ((s8[13107200]{0:T(1024)(128)(4,1)}), s8[4194304]{0:T(1024)(128)(4,1)S(1)}, s32[]{:S(2)}) async-start(s8[13107200]{0:T(1024)(128)(4,1)} %bitcast.104), calls=%async_computation.5 | async-start | bytes 8388608 | tf_op jit(solution)/shard_map/while
  404.0 7.3 %slice-start.1 = ((s8[13107200]{0:T(1024)(128)(4,1)}), s8[4194304]{0:T(1024)(128)(4,1)S(1)}, s32[]{:S(2)}) async-start(s8[13107200]{0:T(1024)(128)(4,1)} %bitcast.104), calls=%async_computation.6 | async-start | bytes 8388608 | tf_op jit(solution)/shard_map/while
  415.0 15.7 %copy-start = (bf16[16,128,32]{1,2,0:T(8,128)(2,1)}, bf16[16,128,32]{1,2,0:T(8,128)(2,1)S(1)}, u32[]{:S(2)}) copy-start(bf16[16,128,32]{1,2,0:T(8,128)(2,1)S(1)} %get-tuple-element.309) | copy-start | bytes 393220
  (50 other events, 181.6 us)
Sparse Core Ops, SparseCore 0:
  9.6 23.8 all-gather.14
  35.1 26.7 all-gather.8
  63.5 34.7 all-gather.10
  99.7 22.0 all-gather.6
  123.3 66.0 all-gather.12
where the time goes:
time: 439 us; the launch traced here: 437 us
  matrix products  206 us (47%)
  waiting for transfers between devices  122 us (28%)
  local copies, waits for them, and re-layouts  40 us (9%)
  other arithmetic  36.9 us (8%)
  between operations  15.9 us (4%)
  blocking collectives  14.1 us (3%)
    dot_general x16, matrix products, attend(): jnp.einsum('btr,rc->btc', q_lat, w_uq, preferred_element_type=jnp.float32)  74.5 us
    all_gather x1, waiting for transfers between devices, local_block(): w_out_all = lax.all_gather(w_out_s, 'fsdp', tiled=True)  67.5 us
    dot_general x16, matrix products, attend(): jnp.einsum('btc,cd->btd', attn_out, w_out, preferred_element_type=jnp.flo...  47.8 us
    dot_general x16, matrix products, attend(): jnp.einsum('btr,rc->btc', latent, w_ukv, preferred_element_type=jnp.float32)  36.7 us
    all_gather x1, waiting for transfers between devices, local_block(): w_uq_all = lax.all_gather(w_uq_s, 'fsdp', tiled=True)  21.6 us
    convert_element_type x1, other arithmetic, local_block(): y_blk = (tok_blk.astype(jnp.float32) + proj_out).astype(jnp.bfloat16)  15.7 us
    all_gather x1, waiting for transfers between devices, local_block(): w_ukv_all = lax.all_gather(w_ukv_s, 'fsdp', tiled=True)  15.1 us
    all_gather x1, waiting for transfers between devices, local_block(): w_dq_all = lax.all_gather(w_dq_s, 'fsdp', tiled=True)  14.4 us
  transfers between devices with their start and end apart: 5, of which 4 were waited for; matrix products, arithmetic and copies ran while one was open for 10% of the time, Pallas kernels for 0%

commit v1 on v0

v1 whole, which is shorter than its diff:
```python
import functools

import jax
import jax.numpy as jnp
import numpy as np
from jax import lax
from jax.experimental import pallas as pl
from jax.experimental.pallas import tpu as pltpu
from jax.sharding import PartitionSpec as P

EPSILON = 1e-6
ROPE_THETA = 10000.0
MESH = pl.DeviceIdType.MESH
BF16 = jnp.bfloat16
F32 = jnp.float32
N_MSG = 14
TILE = 256


def rope_tables(seq_len, rope_dim):
    half_dim = rope_dim // 2
    expo = (-2.0 * np.arange(half_dim, dtype=np.float32) / np.float32(rope_dim)).astype(np.float32)
    inv_freq = np.power(np.float32(ROPE_THETA), expo).astype(np.float32)
    angles = np.arange(seq_len, dtype=np.float32)[:, None] * inv_freq[None, :]
    return np.cos(angles).astype(np.float32), np.sin(angles).astype(np.float32)


def rms(v, gain):
    return v * lax.rsqrt(jnp.mean(v * v, axis=-1, keepdims=True) + EPSILON) * gain


class Item:
    def __init__(self, index, local, full, rows, by_rows, private, col0, cols):
        self.index, self.local, self.full = index, local, full
        self.rows, self.by_rows, self.s = rows, by_rows, private
        self.col0, self.cols = col0, cols
        self.span = rows if by_rows else cols

    def _cut(self, ref, row0, off, size):
        if self.by_rows:
            rows = pl.ds(pl.multiple_of(row0 + off, 16), size)
            cols = pl.ds(self.col0, self.cols)
        else:
            rows = pl.ds(row0 if isinstance(row0, int) else pl.multiple_of(row0, 16), self.rows)
            cols = pl.ds(pl.multiple_of(self.col0 + off, 128), size)
        return ref.at[rows, cols]

    def mine(self, off, size):
        return self._cut(self.local, 0, off, size)

    def at(self, origin, off, size):
        return self._cut(self.full, origin * self.rows, off, size)


def gather_kernel(
    dims, x_hbm, gains_ref, wdq_l, wdkv_l, wuq_l, wukv_l, wo_l, cos_t, sin_t, cos_n, sin_n,
    o_hbm, wo_full, c_hbm, r_hbm,
    gbuf, a_s, wdq, wdkv, acc_q, acc_kv, wuq, wuq_t, wukv, wk, wv_t,
    cq_t, c_s, c_t, r_s, qs, ks, vs, o_s, stage, diff_s,
    ssem, rsem, lsem, gssem, grsem, xsem, osem, csem,
):
    n_dev, n_heads, nope, rope, vdim, d_model, q_rank, kv_rank, seq = dims
    f = lax.axis_index('fsdp')
    d = lax.axis_index('dp')
    core = lax.rem(f, 2)
    par = lax.rem(d, 2)
    chip = f // 2
    n_chip = n_dev // 2
    mod = lambda v: lax.rem(v, n_dev)
    right, left, opp = mod(f + 2), mod(f + n_dev - 2), mod(f + 4)
    partner = f + 1 - 2 * core
    p_right, p_left, p_opp = mod(partner + 2), mod(partner + n_dev - 2), mod(partner + 4)
    d_pair = d + 1 - 2 * par
    to_right, to_left, to_partner, to_pair = (d, right), (d, left), (d, partner), (d_pair, f)
    n_tok = a_s.shape[0]
    n_tile = n_tok // TILE
    half_heads = n_heads // 2
    pairs = half_heads // 2
    hd = nope + rope

    barrier = pltpu.get_barrier_semaphore()
    for step in range(1, n_dev):
        pl.semaphore_signal(barrier, inc=1, device_id=(d, mod(f + step)), device_id_type=MESH)
    pl.semaphore_signal(barrier, inc=1, device_id=to_pair, device_id_type=MESH)
    x_in = [
        pltpu.make_async_copy(x_hbm.at[pl.ds(TILE * t, TILE)], a_s.at[pl.ds(TILE * t, TILE)], xsem.at[t])
        for t in range(n_tile)
    ]
    for cp in x_in:
        cp.start()
    pl.semaphore_wait(barrier, n_dev)

    r_d, r_q, r_kv, r_o = wdq_l.shape[0], wuq_l.shape[0], wukv_l.shape[0], wo_l.shape[0]
    third = lambda n, unit: ((n // unit + 2) // 3) * unit
    items = [
        Item(0, wdq_l, wdq, r_d, True, third(r_d, 16), 0, wdq_l.shape[1]),
        Item(1, wdkv_l, wdkv, r_d, True, third(r_d, 16), 0, wdkv_l.shape[1]),
    ]
    uq_c, ukv_c = wuq_l.shape[1] // 2, wukv_l.shape[1] // 2
    for h in range(2):
        items.append(Item(2 + 2 * h, wuq_l, wuq, r_q, True, third(r_q, 16), h * uq_c, uq_c))
        items.append(Item(3 + 2 * h, wukv_l, wukv, r_kv, False, third(ukv_c, 128), h * ukv_c, ukv_c))
    n_o = 4
    o_c = wo_l.shape[1] // n_o
    for h in range(n_o):
        items.append(Item(6 + h, wo_l, wo_full, r_o, True, third(r_o, 16), h * o_c, o_c))

    def messages(it):
        n, s = it.span, it.s
        own_p, m_off, pm_off, other_p = par * (n - s), s, par * s, (1 - par) * (n - s)
        pm = n - s
        m = n - 2 * s
        reg = it.at
        return [
            (it.mine(pm_off, pm), reg(f, pm_off, pm), to_right, reg(left, pm_off, pm)),
            (it.mine(pm_off, pm), reg(f, pm_off, pm), to_left, reg(right, pm_off, pm)),
            (it.mine(0, n), reg(f, 0, n), to_partner, reg(partner, 0, n)),
            (reg(left, own_p, s), reg(left, own_p, s), to_right, reg(opp, own_p, s)),
            (reg(right, m_off, m), reg(right, m_off, m), to_left, reg(opp, m_off, m)),
            (reg(left, own_p, s), reg(left, own_p, s), to_pair, reg(left, other_p, s)),
            (reg(right, own_p, s), reg(right, own_p, s), to_pair, reg(right, other_p, s)),
            (reg(opp, own_p, s), reg(opp, own_p, s), to_pair, reg(opp, other_p, s)),
            (reg(left, pm_off, pm), reg(left, pm_off, pm), to_partner, reg(p_left, pm_off, pm)),
            (reg(right, pm_off, pm), reg(right, pm_off, pm), to_partner, reg(p_right, pm_off, pm)),
            (reg(opp, pm_off, pm), reg(opp, pm_off, pm), to_partner, reg(p_opp, pm_off, pm)),
            (reg(left, other_p, s), reg(left, other_p, s), to_partner, reg(p_left, other_p, s)),
            (reg(right, other_p, s), reg(right, other_p, s), to_partner, reg(p_right, other_p, s)),
            (reg(opp, other_p, s), reg(opp, other_p, s), to_partner, reg(p_opp, other_p, s)),
        ]

    def send(it, t):
        src, dst, dev, _ = messages(it)[t]
        k = it.index * N_MSG + t
        return pltpu.make_async_remote_copy(src, dst, ssem.at[k], rsem.at[k], device_id=dev, device_id_type=MESH)

    def recv(it, t):
        _, _, dev, got = messages(it)[t]
        k = it.index * N_MSG + t
        return pltpu.make_async_remote_copy(got, got, ssem.at[k], rsem.at[k], device_id=dev, device_id_type=MESH)

    def start(it, *ts):
        for t in ts:
            send(it, t).start()

    def got(it, *ts):
        for t in ts:
            recv(it, t).wait_recv()

    def local_copy(it):
        return pltpu.make_async_copy(it.mine(0, it.span), it.at(f, 0, it.span), lsem.at[it.index])

    stage_in = pltpu.make_async_copy(wo_l, stage, lsem.at[6])
    stage_out = pltpu.make_async_copy(stage, wo_full.at[pl.ds(pl.multiple_of(f * r_o, 16), r_o)], lsem.at[7])

    def step_a(i):
        start(items[i], 0, 1, 2)
        if i < 6:
            local_copy(items[i]).start()

    def step_b(i):
        got(items[i], 0, 1)
        start(items[i], 3, 4, 5, 6, 8, 9)

    def step_c(i):
        got(items[i], 3, 4)
        start(items[i], 7, 10)

    def step_d(i):
        got(items[i], 5, 6)
        start(items[i], 11, 12)

    def step_d2(i):
        got(items[i], 7)
        start(items[i], 13)

    def step_e(i):
        got(items[i], 2, 8, 9, 10, 11, 12, 13)
        if i < 6:
            local_copy(items[i]).wait()

    def gain_copy(step):
        return pltpu.make_async_remote_copy(
            gains_ref, gbuf.at[step - 1], gssem.at[step - 1], grsem.at[step - 1],
            device_id=(d, mod(f + step)), device_id_type=MESH,
        )

    for step in range(1, n_dev):
        gain_copy(step).start()
    step_a(0)
    step_a(1)
    stage_in.start()

    row_i = lax.broadcasted_iota(jnp.int32, (seq, 2 * seq), 0)
    lane_i = lax.broadcasted_iota(jnp.int32, (seq, 2 * seq), 1)
    diff_s[...] = lax.rem(lane_i, seq) - row_i
    for p in range(2):
        @pl.loop(0, pairs)
        def _(j, p=p):
            qs[p, j] = jnp.zeros(qs.shape[2:], BF16)

    @pl.loop(0, pairs)
    def _(j):
        vs[j, 2 * vdim:, :] = jnp.ones((vs.shape[1] - 2 * vdim, vs.shape[2]), BF16)

    r_s[...] = jnp.zeros(r_s.shape, BF16)

    for step in range(1, n_dev):
        gain_copy(step).wait_recv()
    gain = gains_ref[...]
    for step in range(1, n_dev):
        gain = gain + gbuf[step - 1]
    g_in = gain[:, :d_model]
    g_q = gain[:, d_model:d_model + q_rank]
    g_kv = gain[:, d_model + q_rank:]

    for cp in x_in:
        cp.wait()

    @pl.loop(0, n_tok // 64)
    def _(t):
        rows = pl.ds(pl.multiple_of(t * 64, 64), 64)
        a_s[rows, :] = rms(a_s[rows, :].astype(F32), g_in).astype(BF16)

    depth = 2 * r_d

    def down(chip_i, first):
        cols = pl.ds(pl.multiple_of(chip_i * depth, 128), depth)

        @pl.loop(0, n_tile)
        def _(t):
            rows = pl.ds(pl.multiple_of(t * TILE, TILE), TILE)
            a = a_s[rows, cols]
            q = jnp.dot(a, wdq[cols, :], preferred_element_type=F32)
            kv = jnp.dot(a, wdkv[cols, :], preferred_element_type=F32)
            if first:
                acc_q[rows, :] = q
                acc_kv[rows, :] = kv
            else:
                acc_q[rows, :] += q
                acc_kv[rows, :] += kv

    for i in (0, 1):
        got(items[i], 2)
        local_copy(items[i]).wait()
    down(chip, True)
    step_b(0)
    step_b(1)
    step_a(2)
    step_a(3)
    for i in (0, 1):
        step_d(i)
    for i in (0, 1):
        got(items[i], 8, 11)
    down(lax.rem(chip + n_chip - 1, n_chip), False)
    step_c(0)
    step_c(1)
    for i in (0, 1):
        got(items[i], 9, 12)
    down(lax.rem(chip + 1, n_chip), False)
    step_d2(0)
    step_d2(1)
    for i in (0, 1):
        got(items[i], 10, 13)
    down(lax.rem(chip + 2, n_chip), False)
    stage_in.wait()
    stage_out.start()

    @pl.loop(0, n_tile)
    def _(t):
        rows = pl.ds(pl.multiple_of(t * TILE, TILE), TILE)
        cq_t[:, rows] = rms(acc_q[rows, :], g_q).astype(BF16).T
        kv = acc_kv[rows, :]
        lat = rms(kv[:, :kv_rank], g_kv).astype(BF16)
        c_s[rows, :] = lat
        c_t[:, rows] = lat.T
        pe = kv[:, kv_rank:]
        swapped = jnp.concatenate([pe[:, rope // 2:], pe[:, :rope // 2]], axis=1)
        r_s[rows, :rope] = (pe * cos_n[...] + swapped * sin_n[...]).astype(BF16)

    c_out = pltpu.make_async_copy(c_s, c_hbm, csem.at[0])
    r_out = pltpu.make_async_copy(r_s, r_hbm, csem.at[1])
    c_out.start()
    r_out.start()

    step_b(2)
    step_b(3)
    step_a(4)
    step_a(5)
    step_d(2)
    step_d(3)
    step_c(2)
    step_c(3)
    step_d2(2)
    step_d2(3)
    step_e(2)
    step_e(3)

    plan = {
        0: [(step_b, 4), (step_b, 5), (step_a, 6)],
        2: [(step_d, 4), (step_d, 5), (step_c, 4), (step_c, 5)],
        3: [(step_d2, 4), (step_d2, 5)],
        5: [(step_b, 6), (step_a, 7)],
        7: [(step_d, 6), (step_c, 6), (step_e, 4), (step_e, 5)],
        8: [(step_d2, 6)],
        9: [(step_b, 7), (step_a, 8)],
        11: [(step_d, 7), (step_c, 7)],
        12: [(step_d2, 7)],
        13: [(step_b, 8), (step_a, 9)],
        15: [(step_d, 8), (step_c, 8)],
    }
    scale = float((nope + rope) ** -0.5)
    exp_scale = scale * float(np.log2(np.e))
    fill = -1e30 / scale
    cos_q, sin_q = cos_t[...], sin_t[...]
    hr = rope // 2

    def o_copy(slot, t, h):
        return pltpu.make_async_copy(
            o_s.at[slot],
            o_hbm.at[pl.ds(pl.multiple_of(t * TILE, TILE), TILE),
                     pl.ds(pl.multiple_of(h * half_heads * vdim, 128), half_heads * vdim)],
            osem.at[slot],
        )

    chunk = 4

    @pl.loop(0, 2)
    def _(h):
        for b in range(uq_c // 128):
            cols = pl.ds(pl.multiple_of(h * uq_c + b * 128, 128), 128)
            wuq_t[b * 128:(b + 1) * 128, :] = wuq[:, cols].T
        for j in range(pairs):
            c0 = h * ukv_c + j * 2 * (nope + vdim)
            wa = wukv[:, pl.ds(pl.multiple_of(c0, 128), nope + vdim)]
            wb = wukv[:, pl.ds(pl.multiple_of(c0 + nope + vdim, 128), nope + vdim)]
            wk[:, 2 * nope * j:2 * nope * (j + 1)] = jnp.concatenate([wa[:, :nope], wb[:, :nope]], axis=1)
            wv_t[2 * vdim * j:2 * vdim * (j + 1), :] = jnp.concatenate([wa.T[nope:], wb.T[nope:]], axis=0)

        @pl.loop(0, n_tile)
        def _(t):
            it = h * n_tile + t
            for when, todo in plan.items():
                @pl.when(it == when)
                def _(todo=todo):
                    for fn, i in todo:
                        fn(i)
            slot = lax.rem(it, 2)
            rows = pl.ds(pl.multiple_of(t * TILE, TILE), TILE)
            cq = cq_t[:, rows]
            for g in range(half_heads // chunk):
                w = wuq_t[g * chunk * hd:(g + 1) * chunk * hd, :]
                q = jnp.dot(w, cq, preferred_element_type=F32)
                for hh in range(chunk):
                    j, side = (g * chunk + hh) // 2, hh % 2
                    r0 = hh * hd
                    for p in range(2):
                        lanes = slice(seq * p, seq * (p + 1))
                        dst = slice(seq * side, seq * (side + 1))
                        qs[p, j, side * nope:(side + 1) * nope, dst] = q[r0:r0 + nope, lanes].astype(BF16)
                        lo = q[r0 + nope:r0 + nope + hr, lanes]
                        hi = q[r0 + nope + hr:r0 + hd, lanes]
                        qs[p, j, 2 * nope:2 * nope + hr, dst] = (lo * cos_q - hi * sin_q).astype(BF16)
                        qs[p, j, 2 * nope + hr:2 * nope + rope, dst] = (hi * cos_q + lo * sin_q).astype(BF16)
            lat = c_s[rows, :]
            ks[...] = jnp.dot(lat, wk[...], preferred_element_type=F32).astype(BF16)
            v = jnp.dot(wv_t[...], c_t[:, rows], preferred_element_type=F32).astype(BF16)
            for j in range(pairs):
                vs[j, :2 * vdim, :] = v[2 * vdim * j:2 * vdim * (j + 1)]

            @pl.when(it >= 2)
            def _():
                o_copy(slot, t, h).wait()

            for p in range(2):
                r_blk = r_s[pl.ds(pl.multiple_of(t * TILE + p * seq, seq), seq), :]
                for j in range(pairs):
                    lhs = jnp.concatenate([ks[seq * p:seq * (p + 1), 2 * nope * j:2 * nope * (j + 1)], r_blk], axis=1)
                    s = jnp.dot(lhs, qs[p, j], preferred_element_type=F32)
                    s = jnp.where(diff_s[...] >= 0, s, fill)
                    m = jnp.max(s, axis=0, keepdims=True)
                    e = jnp.exp2((s - m) * exp_scale).astype(BF16)
                    ov = jnp.dot(vs[j, :, seq * p:seq * (p + 1)], e, preferred_element_type=F32)
                    inv = 1.0 / ov[2 * vdim:2 * vdim + 1, :]
                    oa = ov[:vdim, :seq] * inv[:, :seq]
                    ob = ov[vdim:2 * vdim, seq:] * inv[:, seq:]
                    o_t = jnp.concatenate([oa, ob], axis=0).astype(BF16)
                    o_s[slot, seq * p:seq * (p + 1), 2 * vdim * j:2 * vdim * (j + 1)] = o_t.T
            o_copy(slot, t, h).start()

    step_d2(8)
    step_b(9)
    step_d(9)
    step_c(9)
    step_d2(9)
    for i in range(6, 6 + n_o):
        step_e(i)
    stage_out.wait()
    o_copy(0, n_tile - 2, 1).wait()
    o_copy(1, n_tile - 1, 1).wait()
    c_out.wait()
    r_out.wait()
    for step in range(1, n_dev):
        gain_copy(step).wait_send()
    for it in items:
        for t in range(N_MSG):
            send(it, t).wait_send()


def out_kernel(o_ref, w_ref, x_ref, c_ref, r_ref, y_ref, c_out, r_out):
    acc = jnp.dot(o_ref[...], w_ref[...], preferred_element_type=F32)
    y_ref[...] = (x_ref[...].astype(F32) + acc).astype(BF16)
    c_out[...] = c_ref[...]
    r_out[...] = r_ref[:, :r_out.shape[1]]


def solution(mesh):
    batch_spec = P(('dp', 'fsdp'))
    row_spec = P('fsdp')
    mat_spec = P('fsdp', None)
    n_dev = mesh.shape['fsdp']
    assert n_dev == 8 and mesh.shape['dp'] % 2 == 0

    def local_block(tok, g_in, w_dq, g_q, w_uq, w_dkv, g_kv, w_ukv, w_out):
        n_p, seq, d_model = tok.shape
        n_tok = n_p * seq
        kv_rank, q_rank = g_kv.shape[0] * n_dev, g_q.shape[0] * n_dev
        rope = w_dkv.shape[1] - kv_rank
        nope_total = w_ukv.shape[1] - w_out.shape[0] * n_dev
        n_heads = (w_uq.shape[1] - nope_total) // rope
        nope = nope_total // n_heads
        vdim = w_out.shape[0] * n_dev // n_heads
        pairs = n_heads // 4
        hh = n_heads // 2
        x2 = tok.reshape(n_tok, d_model)
        me = lax.axis_index('fsdp')

        def spread(g, total):
            return lax.dynamic_update_slice(jnp.zeros((total,), F32), g.astype(F32), (me * g.shape[0],))

        gains = jnp.concatenate([spread(g_in, d_model), spread(g_q, q_rank), spread(g_kv, kv_rank)])[None]
        cos, sin = rope_tables(seq, rope)
        cos_t, sin_t = jnp.asarray(cos.T), jnp.asarray(sin.T)
        reps = TILE // seq
        cos_n = jnp.asarray(np.tile(np.concatenate([cos, cos], 1), (reps, 1)))
        sin_n = jnp.asarray(np.tile(np.concatenate([-sin, sin], 1), (reps, 1)))
        dims = (n_dev, n_heads, nope, rope, vdim, d_model, q_rank, kv_rank, seq)
        n_items = 10
        any_ = pl.BlockSpec(memory_space=pl.ANY)
        vm = pl.BlockSpec(memory_space=pltpu.VMEM)
        o, wo_full, c_all, r_all = pl.pallas_call(
            functools.partial(gather_kernel, dims),
            out_shape=(
                jax.ShapeDtypeStruct((n_tok, n_heads * vdim), BF16),
                jax.ShapeDtypeStruct((n_heads * vdim, d_model), BF16),
                jax.ShapeDtypeStruct((n_tok, kv_rank), BF16),
                jax.ShapeDtypeStruct((n_tok, 128), BF16),
            ),
            in_specs=[any_, vm] + [any_] * 5 + [vm] * 4,
            out_specs=(any_,) * 4,
            scratch_shapes=[
                pltpu.VMEM((n_dev - 1, 1, gains.shape[1]), F32),
                pltpu.VMEM((n_tok, d_model), BF16),
                pltpu.VMEM((d_model, q_rank), BF16),
                pltpu.VMEM((d_model, kv_rank + rope), BF16),
                pltpu.VMEM((n_tok, q_rank), F32),
                pltpu.VMEM((n_tok, kv_rank + rope), F32),
                pltpu.VMEM((q_rank, w_uq.shape[1]), BF16),
                pltpu.VMEM((w_uq.shape[1] // 2, q_rank), BF16),
                pltpu.VMEM((kv_rank, w_ukv.shape[1]), BF16),
                pltpu.VMEM((kv_rank, hh * nope), BF16),
                pltpu.VMEM((hh * vdim, kv_rank), BF16),
                pltpu.VMEM((q_rank, n_tok), BF16),
                pltpu.VMEM((n_tok, kv_rank), BF16),
                pltpu.VMEM((kv_rank, n_tok), BF16),
                pltpu.VMEM((n_tok, 128), BF16),
                pltpu.VMEM((2, pairs, 2 * nope + 128, 2 * seq), BF16),
                pltpu.VMEM((TILE, hh * nope), BF16),
                pltpu.VMEM((pairs, 2 * vdim + 16, TILE), BF16),
                pltpu.VMEM((2, TILE, hh * vdim), BF16),
                pltpu.VMEM(w_out.shape, BF16),
                pltpu.VMEM((seq, 2 * seq), jnp.int32),
                pltpu.SemaphoreType.DMA((n_items * N_MSG,)),
                pltpu.SemaphoreType.DMA((n_items * N_MSG,)),
                pltpu.SemaphoreType.DMA((8,)),
                pltpu.SemaphoreType.DMA((n_dev - 1,)),
                pltpu.SemaphoreType.DMA((n_dev - 1,)),
                pltpu.SemaphoreType.DMA((n_tok // TILE,)),
                pltpu.SemaphoreType.DMA((2,)),
                pltpu.SemaphoreType.DMA((2,)),
            ],
            compiler_params=pltpu.CompilerParams(
                collective_id=0, has_side_effects=True, vmem_limit_bytes=67_043_328
            ),
            name='gather_attend',
        )(x2, gains, w_dq, w_dkv, w_uq, w_ukv, w_out, cos_t, sin_t, cos_n, sin_n)

        bm, bn = 512, 512
        n_m, n_n = n_tok // bm, d_model // bn
        once = lambda n, m: (jnp.where(n == 0, m, n_m - 1), 0)
        y, c_blk, r_blk = pl.pallas_call(
            out_kernel,
            grid=(n_n, n_m),
            in_specs=[
                pl.BlockSpec((bm, n_heads * vdim), lambda n, m: (m, 0)),
                pl.BlockSpec((n_heads * vdim, bn), lambda n, m: (0, n)),
                pl.BlockSpec((bm, bn), lambda n, m: (m, n)),
                pl.BlockSpec((bm, kv_rank), once),
                pl.BlockSpec((bm, 128), once),
            ],
            out_specs=[
                pl.BlockSpec((bm, bn), lambda n, m: (m, n)),
                pl.BlockSpec((bm, kv_rank), once),
                pl.BlockSpec((bm, rope), once),
            ],
            out_shape=[
                jax.ShapeDtypeStruct((n_tok, d_model), BF16),
                jax.ShapeDtypeStruct((n_tok, kv_rank), BF16),
                jax.ShapeDtypeStruct((n_tok, rope), BF16),
            ],
            compiler_params=pltpu.CompilerParams(vmem_limit_bytes=48 * 1024 * 1024),
            name='project_out',
        )(o, wo_full, x2, c_all, r_all)
        return y.reshape(tok.shape), c_blk.reshape(n_p, seq, kv_rank), r_blk.reshape(n_p, seq, rope)

    return jax.shard_map(
        local_block,
        mesh=mesh,
        in_specs=(batch_spec, row_spec, mat_spec, row_spec, mat_spec, mat_spec, row_spec, mat_spec, mat_spec),
        out_specs=(batch_spec, batch_spec, batch_spec),
        check_vma=False,
    )
```

time: 439 us -> 216 us (0.49)
  Pallas kernels: 0 us -> 207 us
  matrix products: 206 us -> 0 us
  waiting for transfers between devices: 122 us -> 0 us
  other arithmetic: 36.9 us -> 2.27 us
  local copies, waits for them, and re-layouts: 40 us -> 5.5 us
  between operations: 15.9 us -> 0.66 us
  blocking collectives: 14.1 us -> 0 us
    pallas_call x0 -> x2, Pallas kernels: none -> 207 us  [the longest x1 164 us: local_block(): pl.pallas_call(functools.partial(gather_kernel, dims), out_shape=(jax.Sha...]
    dot_general x98 -> x0, matrix products: 206 us -> none  [the longest x16 74.5 us: attend(): jnp.einsum('btr,rc->btc', q_lat, w_uq, preferred_element_type=jnp.float32)]
    all_gather x5 -> x0, waiting for transfers between devices: 119 us -> none  [the longest x1 67.5 us: local_block(): w_out_all = lax.all_gather(w_out_s, 'fsdp', tiled=True)]
    convert_element_type x6 -> x0, other arithmetic: 18.2 us -> none  [the longest x1 15.7 us: local_block(): y_blk = (tok_blk.astype(jnp.float32) + proj_out).astype(jnp.bfloat16)]
    reduce_sum x18 -> x0, other arithmetic: 14.8 us -> none  [the longest x16 8.58 us: attend(): attn_probs = jax.nn.softmax(scores, axis=-1).astype(jnp.bfloat16)]
    unnamed x1 -> x0, blocking collectives: 14.1 us -> none
    reshape x16 -> x0, local copies, waits for them, and re-layouts: 12.5 us -> none  [attend(): kv_up = kv_up.reshape(n_prompts, seq_len, n_heads, nope_dim + v_dim)]
    while x128 -> x0, local copies, waits for them, and re-layouts: 12 us -> none
  transfers between devices with their start and end apart: 5 -> 0, of which waited for: 4 -> 0; matrix products, arithmetic and copies ran while one was open for 10% -> 0% of each run, Pallas kernels for 0% -> 0%
where the time goes in v1:
time: 216 us; the launch traced here: 215 us
  Pallas kernels  207 us (96%)
  local copies, waits for them, and re-layouts  5.5 us (3%)
  other arithmetic  2.27 us (1%)
    pallas_call x1, Pallas kernels, local_block(): pl.pallas_call(functools.partial(gather_kernel, dims), out_shape=(jax.Sha...  164 us
    pallas_call x1, Pallas kernels, local_block(): pl.pallas_call(out_kernel, grid=(n_n, n_m), in_specs=[pl.BlockSpec((bm, n...  42.8 us
    unnamed x6, local copies, waits for them, and re-layouts  4.89 us

profile of v1, /device:TPU:113, one launch (start us, length us, event | category | flops | bytes accessed | tf_op | source)
XLA Modules:
  0.0 215.4 jit_solution(16837282285318628027)
XLA Ops:
  0.6 0.8 convert_dynamic-update-slice_fusion.1
  1.4 0.7 convert_dynamic-update-slice_fusion.2
  2.1 0.8 convert_dynamic-update-slice_fusion
  2.9 0.6 broadcast_in_dim.15.gains_ref
  3.5 1.8 copy.16.wdkv_l
  5.3 164.1 %gather_attend.1 = (bf16[2048,2560]{1,0:T(8,128)(2,1)}, bf16[2560,2560]{1,0:T(8,128)(2,1)}, bf16[2048,256]{1,0:T(8,128)(2,1)}, bf16[2048,128]{1,0:T(8,128)(2,1)}) custom-call(bf16[2048,2560]{1,0:T(8,128)(2,1)} %bitcast.5, f32[1,3584]{1,0:T(1,128)} %broadcast_in_dim.15.gains_ref, bf16[320,768]{1,0:T(8,128)(2,1)} %wdq_l.1, bf16[320,288]{1,0:T(8,128)(2,1)} %copy.16.wdkv_l, ...), custom_call_target="tpu_custom_call" | custom-call | tf_op jit(solution)/shard_map/gather_attend/pallas_call | solution.py:450
  169.5 0.0 copy-start
  169.5 1.2 copy-done
  170.7 0.0 copy-start.1
  170.7 1.0 copy-done.1
  171.7 42.8 %project_out.1 = (bf16[2048,2560]{1,0:T(8,128)(2,1)}, bf16[2048,256]{1,0:T(8,128)(2,1)}, bf16[2048,32]{1,0:T(8,128)(2,1)S(1)}) custom-call(bf16[2048,2560]{1,0:T(8,128)(2,1)} %get-tuple-element.10.o_ref, bf16[2560,2560]{1,0:T(8,128)(2,1)} %get-tuple-element.11.w_ref, bf16[2048,2560]{1,0:T(8,128)(2,1)} %bitcast.6, bf16[2048,256]{1,0:T(8,128)(2,1)S(1)} %copy-done, ...), custom_call_target="tpu_custom_call" | custom-call | tf_op jit(solution)/shard_map/project_out/pallas_call | solution.py:500
  214.5 0.8 copy.17
  (4 shorter events, 0.0 us)
Async XLA Ops:
  169.5 1.2 copy-start
  170.7 1.0 copy-start.1

commit v2 on v1

v2 whole, which is shorter than its diff:
```python
import functools

import jax
import jax.numpy as jnp
import numpy as np
from jax import lax
from jax.experimental import pallas as pl
from jax.experimental.pallas import tpu as pltpu
from jax.sharding import PartitionSpec as P

EPSILON = 1e-6
ROPE_THETA = 10000.0
MESH = pl.DeviceIdType.MESH
BF16 = jnp.bfloat16
F32 = jnp.float32
N_MSG = 14
TILE = 256
NORM = 128


def rope_tables(seq_len, rope_dim):
    half_dim = rope_dim // 2
    expo = (-2.0 * np.arange(half_dim, dtype=np.float32) / np.float32(rope_dim)).astype(np.float32)
    inv_freq = np.power(np.float32(ROPE_THETA), expo).astype(np.float32)
    angles = np.arange(seq_len, dtype=np.float32)[:, None] * inv_freq[None, :]
    return np.cos(angles).astype(np.float32), np.sin(angles).astype(np.float32)


def rms(v, gain):
    return v * lax.rsqrt(jnp.mean(v * v, axis=-1, keepdims=True) + EPSILON) * gain


THEN = {0: (3, 5, 8), 1: (4, 6, 9), 3: (7,), 4: (10,), 5: (11,), 6: (12,), 7: (13,)}
ROUTE = 'RLDRLZZZDDDDDD'
SPLITS = ((112, 160), (32, 48), (64, 128), (32, 32), (512, 768), (32, 48), (896, 896),
          (96, 128), (80, 112), (96, 112), (48, 80))
T_NORM, T_DOWN, T_PREP, T_ITER = 6.0, 2.6, 1.9, 2.7


def plan_transfers(pieces, steps):
    rate = {'R': 46.6e3, 'L': 46.6e3, 'Z': 46.6e3, 'D': 300e3}
    hop = {'R': 2.3, 'L': 2.3, 'Z': 2.3, 'D': 1.5}
    free = dict.fromkeys(rate, 0.0)
    state = {'now': 2.5, 'next': 0}
    arrival, done, lists = {}, set(), []

    def send(i, t):
        n, p, r, unit = pieces[i]
        pm = n - p
        size = (pm, pm, n, r, pm - r, p, p, p, pm, pm, pm, p, p, p)[t] * unit
        link = ROUTE[t]
        free[link] = max(state['now'], free[link]) + size / rate[link]
        arrival[i, t] = free[link] + hop[link]

    def own(out):
        i = state['next']
        state['next'] = i + 1
        for t in (0, 1, 2):
            send(i, t)
        out.append((i, -1))

    def wait(i, t, out):
        state['now'] = max(state['now'], arrival[i, t])
        done.add((i, t))
        out.append((i, t))
        for u in THEN.get(t, ()):
            send(i, u)

    for k, (need, busy) in enumerate(steps):
        out = []
        while True:
            while state['next'] < len(pieces) and (
                k == 0 and state['next'] < 3 or min(free['R'], free['L']) - state['now'] < 4
            ):
                own(out)
            ready = sorted(
                (a, i, t) for (i, t), a in arrival.items()
                if (i, t) not in done and t in THEN and (t != 4 or (i, 3) in done)
            )
            if ready and ready[0][0] + 0.3 <= state['now']:
                wait(*ready[0][1:], out)
                continue
            missing = [m for m in need if m not in done]
            if not missing:
                break
            here = [m for m in missing if m in arrival and arrival[m] <= state['now']]
            if here:
                wait(*here[0], out)
                continue
            ready += [(arrival[m], *m) for m in missing if m in arrival and m[1] not in THEN]
            wait(*min(ready)[1:], out)
        lists.append(out)
        state['now'] += busy
    return lists


class Item:
    def __init__(self, index, local, full, rows, by_rows, split, col0, cols):
        self.index, self.local, self.full = index, local, full
        self.rows, self.by_rows = rows, by_rows
        self.s, self.h = split
        self.col0, self.cols = col0, cols
        self.span = rows if by_rows else cols

    def _cut(self, ref, row0, off, size):
        if self.by_rows:
            rows = pl.ds(pl.multiple_of(row0 + off, 16), size)
            cols = pl.ds(self.col0, self.cols)
        else:
            rows = pl.ds(row0 if isinstance(row0, int) else pl.multiple_of(row0, 16), self.rows)
            cols = pl.ds(pl.multiple_of(self.col0 + off, 128), size)
        return ref.at[rows, cols]

    def mine(self, off, size):
        return self._cut(self.local, 0, off, size)

    def at(self, origin, off, size):
        return self._cut(self.full, origin * self.rows, off, size)


def gather_kernel(
    dims, x_hbm, gains_hbm, wdq_l, wdkv_l, wuq_l, wukv_l, wo_l, cos_t, sin_t, cos_n, sin_n,
    o_hbm, wo_full, c_hbm, r_hbm,
    gbuf, a_s, wdq, wdkv, acc_q, acc_kv, wuq, wuq_t, wukv, wk, wv_t,
    cq_t, c_s, c_t, r_s, qs, ks, vs, o_s, stage, diff_s, inv_s, gb_s, s_buf, pm, ms,
    ssem, rsem, lsem, gssem, grsem, xsem, osem, csem,
):
    n_dev, n_heads, nope, rope, vdim, d_model, q_rank, kv_rank, seq = dims
    f = lax.axis_index('fsdp')
    d = lax.axis_index('dp')
    core = lax.rem(f, 2)
    par = lax.rem(d, 2)
    chip = f // 2
    n_chip = n_dev // 2
    mod = lambda v: lax.rem(v, n_dev)
    right, left, opp = mod(f + 2), mod(f + n_dev - 2), mod(f + 4)
    partner = f + 1 - 2 * core
    p_right, p_left, p_opp = mod(partner + 2), mod(partner + n_dev - 2), mod(partner + 4)
    d_pair = d + 1 - 2 * par
    to_right, to_left, to_partner, to_pair = (d, right), (d, left), (d, partner), (d_pair, f)
    n_tok = a_s.shape[0]
    n_tile = n_tok // TILE
    half_heads = n_heads // 2
    pairs = half_heads // 2
    hd = nope + rope

    barrier = pltpu.get_barrier_semaphore()
    for step in range(1, n_dev):
        pl.semaphore_signal(barrier, inc=1, device_id=(d, mod(f + step)), device_id_type=MESH)
    pl.semaphore_signal(barrier, inc=1, device_id=to_pair, device_id_type=MESH)
    x_in = [
        pltpu.make_async_copy(x_hbm.at[pl.ds(TILE * t, TILE)], a_s.at[pl.ds(TILE * t, TILE)], xsem.at[t])
        for t in range(n_tile)
    ]
    for cp in x_in:
        cp.start()
    gain_in = pltpu.make_async_copy(gains_hbm, gbuf.at[f], lsem.at[9])
    gain_in.start()
    pl.semaphore_wait(barrier, n_dev)

    r_d, r_q, r_kv, r_o = wdq_l.shape[0], wuq_l.shape[0], wukv_l.shape[0], wo_l.shape[0]
    n_d, n_o = 2, 4
    dq_c, uq_c, ukv_c, o_c = wdq_l.shape[1] // n_d, wuq_l.shape[1] // 2, wukv_l.shape[1] // 2, wo_l.shape[1] // n_o
    parts = [(wdq_l, wdq, r_d, True, h * dq_c, dq_c) for h in range(n_d)]
    parts.append((wdkv_l, wdkv, r_d, True, 0, wdkv_l.shape[1]))
    n_down = len(parts)
    for h in range(2):
        parts.append((wuq_l, wuq, r_q, True, h * uq_c, uq_c))
        parts.append((wukv_l, wukv, r_kv, False, h * ukv_c, ukv_c))
    n_head = len(parts)
    parts += [(wo_l, wo_full, r_o, True, h * o_c, o_c) for h in range(n_o)]
    items = [Item(k, *p[:4], SPLITS[k], *p[4:]) for k, p in enumerate(parts)]

    everything = range(N_MSG)
    needs = lambda lo, hi, ts=everything: [(i, t) for i in range(lo, hi) for t in ts]
    steps = [([], T_NORM), ([], T_NORM)]
    steps += [(needs(0, n_down, (2,)), T_DOWN), ([], T_DOWN)]
    steps += [(needs(0, n_down, (0, 1, 5, 6, 8, 9, 11, 12)), 2 * T_DOWN), ([], 2 * T_DOWN)]
    steps += [(needs(0, n_down), 1.2 * T_DOWN), ([], 1.2 * T_DOWN)]
    first_iter = len(steps) + 1
    for h in range(2):
        for t in range(n_tile):
            need = needs(n_down + 2 * h, n_down + 2 * h + 2) if t == 0 else []
            steps.append((need, T_ITER + (T_PREP if t == 0 else 0)))
    steps.append((needs(n_head, len(parts)), 0))
    pieces = [
        (it.span, it.s, it.h, 2 * (-(-it.cols // 128) * 128 if it.by_rows else it.rows)) for it in items
    ]
    plan = plan_transfers(pieces, [([], 0)] + steps)

    def messages(it):
        n, s, h = it.span, it.s, it.h
        own_p, pm_off, other_p = par * (n - s), par * s, (1 - par) * (n - s)
        pm, m = n - s, n - s - h
        h_off, m_off = par * (n - h), (1 - par) * h + par * s
        reg = it.at
        return [
            (it.mine(pm_off, pm), reg(f, pm_off, pm), to_right, reg(left, pm_off, pm)),
            (it.mine(pm_off, pm), reg(f, pm_off, pm), to_left, reg(right, pm_off, pm)),
            (it.mine(0, n), reg(f, 0, n), to_partner, reg(partner, 0, n)),
            (reg(left, h_off, h), reg(left, h_off, h), to_right, reg(opp, h_off, h)),
            (reg(right, m_off, m), reg(right, m_off, m), to_left, reg(opp, m_off, m)),
            (reg(left, own_p, s), reg(left, own_p, s), to_pair, reg(left, other_p, s)),
            (reg(right, own_p, s), reg(right, own_p, s), to_pair, reg(right, other_p, s)),
            (reg(opp, own_p, s), reg(opp, own_p, s), to_pair, reg(opp, other_p, s)),
            (reg(left, pm_off, pm), reg(left, pm_off, pm), to_partner, reg(p_left, pm_off, pm)),
            (reg(right, pm_off, pm), reg(right, pm_off, pm), to_partner, reg(p_right, pm_off, pm)),
            (reg(opp, pm_off, pm), reg(opp, pm_off, pm), to_partner, reg(p_opp, pm_off, pm)),
            (reg(left, other_p, s), reg(left, other_p, s), to_partner, reg(p_left, other_p, s)),
            (reg(right, other_p, s), reg(right, other_p, s), to_partner, reg(p_right, other_p, s)),
            (reg(opp, other_p, s), reg(opp, other_p, s), to_partner, reg(p_opp, other_p, s)),
        ]

    def send(it, t):
        src, dst, dev, _ = messages(it)[t]
        k = it.index * N_MSG + t
        return pltpu.make_async_remote_copy(src, dst, ssem.at[k], rsem.at[k], device_id=dev, device_id_type=MESH)

    def recv(it, t):
        _, _, dev, got = messages(it)[t]
        k = it.index * N_MSG + t
        return pltpu.make_async_remote_copy(got, got, ssem.at[k], rsem.at[k], device_id=dev, device_id_type=MESH)

    def start(it, *ts):
        for t in ts:
            send(it, t).start()

    def got(it, *ts):
        for t in ts:
            recv(it, t).wait_recv()

    def local_copy(it):
        return pltpu.make_async_copy(it.mine(0, it.span), it.at(f, 0, it.span), lsem.at[it.index])

    stage_in = pltpu.make_async_copy(wo_l, stage, lsem.at[n_head])
    stage_out = pltpu.make_async_copy(stage, wo_full.at[pl.ds(pl.multiple_of(f * r_o, 16), r_o)], lsem.at[n_head + 1])

    def pump(segment):
        for i, t in segment:
            it = items[i]
            if t < 0:
                start(it, 0, 1, 2)
                if i < n_head:
                    local_copy(it).start()
            else:
                got(it, t)
                start(it, *THEN.get(t, ()))

    def own_rows(first, last):
        for i in range(first, last):
            local_copy(items[i]).wait()

    def gain_copy(step):
        return pltpu.make_async_remote_copy(
            gbuf.at[f], gbuf.at[f], gssem.at[step - 1], grsem.at[step - 1],
            device_id=(d, mod(f + step)), device_id_type=MESH,
        )

    gain_in.wait()
    for step in range(1, n_dev):
        gain_copy(step).start()
    pump(plan[0])
    stage_in.start()

    row_i = lax.broadcasted_iota(jnp.int32, (seq, 2 * seq), 0)
    lane_i = lax.broadcasted_iota(jnp.int32, (seq, 2 * seq), 1)
    diff_s[...] = lax.rem(lane_i, seq) - row_i
    for p in range(2):
        @pl.loop(0, pairs)
        def _(j, p=p):
            qs[p, j] = jnp.zeros(qs.shape[2:], BF16)

    @pl.loop(0, pairs)
    def _(j):
        for b in range(2):
            vs[b, j, :2 * vdim, :] = jnp.zeros((2 * vdim, vs.shape[3]), BF16)
            vs[b, j, 2 * vdim:, :] = jnp.ones((vs.shape[2] - 2 * vdim, vs.shape[3]), BF16)
        s_buf[1, j] = jnp.zeros(s_buf.shape[2:], F32)

    r_s[...] = jnp.zeros(r_s.shape, BF16)
    ms[...] = jnp.zeros(ms.shape, F32)

    for t, cp in enumerate(x_in):
        cp.wait()
        v = a_s[TILE * t:TILE * (t + 1), :].astype(F32)
        inv_s[TILE * t:TILE * (t + 1), :] = lax.rsqrt(jnp.mean(v * v, axis=-1, keepdims=True) + EPSILON)

    for step in range(1, n_dev):
        gain_copy(step).wait_recv()
    n_in, n_q, n_kv = d_model // n_dev, q_rank // n_dev, kv_rank // n_dev
    join = lambda lo, n: jnp.concatenate([gbuf[i][:, lo:lo + n] for i in range(n_dev)], axis=1)
    g_in, g_q, g_kv = join(0, n_in), join(n_in, n_q), join(n_in + n_q, n_kv)

    gb_s[...] = jnp.broadcast_to(g_in, gb_s.shape)
    pump(plan[1])

    @pl.loop(0, n_tok // NORM)
    def _(t):
        rows = pl.ds(pl.multiple_of(t * NORM, NORM), NORM)
        v = a_s[rows, :].astype(F32) * inv_s[rows, :]
        v = v.reshape(NORM // 8, 8, d_model) * gb_s[...][None]
        a_s[rows, :] = v.reshape(NORM, d_model).astype(BF16)

    pump(plan[2])

    depth = 2 * r_d

    chip_cols = lambda c: pl.ds(pl.multiple_of(lax.rem(chip + c, n_chip) * depth, 128), depth)
    tile_rows = lambda t: pl.ds(pl.multiple_of(t * TILE, TILE), TILE)

    def down(t, hops):
        rows = tile_rows(t)
        cols = [chip_cols(c) for c in hops]
        a = jnp.concatenate([a_s[rows, c] for c in cols], axis=1)
        for w, acc in ((wdq, acc_q), (wdkv, acc_kv)):
            part = jnp.dot(a, jnp.concatenate([w[c, :] for c in cols], axis=0), preferred_element_type=F32)
            if hops[0] == 0:
                acc[rows, :] = part
            else:
                acc[rows, :] += part

    def finish(t):
        rows = tile_rows(t)
        cq_t[:, rows] = rms(acc_q[rows, :], g_q).astype(BF16).T
        kv = acc_kv[rows, :]
        lat = rms(kv[:, :kv_rank], g_kv).astype(BF16)
        c_s[rows, :] = lat
        c_t[:, rows] = lat.T
        pe = kv[:, kv_rank:]
        swapped = jnp.concatenate([pe[:, rope // 2:], pe[:, :rope // 2]], axis=1)
        r_s[rows, :rope] = (pe * cos_n[...] + swapped * sin_n[...]).astype(BF16)

    own_rows(0, n_down)
    for k, hops in enumerate(((0,), (n_chip - 1, 1))):
        pump(plan[3 + 2 * k])

        @pl.loop(0, n_tile)
        def _(t):
            @pl.when(t == n_tile // 2)
            def _():
                pump(plan[4 + 2 * k])
            down(t, hops)

    pump(plan[7])
    down(0, (2,))

    @pl.loop(1, n_tile)
    def _(t):
        @pl.when(t == n_tile // 2)
        def _():
            pump(plan[8])
        down(t, (2,))
        finish(t - 1)

    finish(n_tile - 1)
    stage_in.wait()
    stage_out.start()
    c_out = pltpu.make_async_copy(c_s, c_hbm, csem.at[0])
    r_out = pltpu.make_async_copy(r_s, r_hbm, csem.at[1])
    c_out.start()
    r_out.start()

    scale = float((nope + rope) ** -0.5)
    exp_scale = scale * float(np.log2(np.e))
    fill = -1e30 / scale
    cos_q, sin_q = cos_t[...], sin_t[...]
    hr = rope // 2

    def o_copy(it):
        h, t, slot = it // n_tile, it % n_tile, it % 3
        return pltpu.make_async_copy(
            o_s.at[slot],
            o_hbm.at[pl.ds(pl.multiple_of(t * TILE, TILE), TILE),
                     pl.ds(pl.multiple_of(h * half_heads * vdim, 128), half_heads * vdim)],
            osem.at[slot],
        )

    groups = seq // 8

    def maxima(p):
        for side in range(2):
            base = 16 * pairs * side + 8 * pairs * p
            part = [pm[pl.ds(base + i, pairs, stride=8), :] for i in range(8)]
            ms[pairs * p:pairs * (p + 1), seq * side:seq * (side + 1)] = functools.reduce(jnp.maximum, part)

    def values(p, j, slot, o_slot):
        k = p * pairs + j
        m = jnp.broadcast_to(ms[k:k + 1, :], (8, 2 * seq))
        s = s_buf[p, j].reshape(groups, 8, 2 * seq)
        e = jnp.exp2((s - m[None]) * exp_scale).astype(BF16).reshape(seq, 2 * seq)
        ov = jnp.dot(vs[slot, j, :, seq * p:seq * (p + 1)], e, preferred_element_type=F32)
        inv = (1.0 / ov[2 * vdim:2 * vdim + 8, :])[None]
        oa = ov[:vdim, :seq].reshape(vdim // 8, 8, seq) * inv[:, :, :seq]
        ob = ov[vdim:2 * vdim, seq:].reshape(vdim // 8, 8, seq) * inv[:, :, seq:]
        o_t = jnp.concatenate([oa, ob], axis=0).reshape(2 * vdim, seq).astype(BF16)
        o_s[o_slot, seq * p:seq * (p + 1), 2 * vdim * j:2 * vdim * (j + 1)] = o_t.T

    chunk = 4

    @pl.loop(0, 2)
    def _(h):
        for k in range(2):
            @pl.when(h == k)
            def _(k=k):
                pump(plan[first_iter + k * n_tile])
                own_rows(n_down + 2 * k, n_down + 2 * k + 2)
        for b in range(uq_c // 128):
            cols = pl.ds(pl.multiple_of(h * uq_c + b * 128, 128), 128)
            wuq_t[b * 128:(b + 1) * 128, :] = wuq[:, cols].T
        for j in range(pairs):
            c0 = h * ukv_c + j * 2 * (nope + vdim)
            wa = wukv[:, pl.ds(pl.multiple_of(c0, 128), nope + vdim)]
            wb = wukv[:, pl.ds(pl.multiple_of(c0 + nope + vdim, 128), nope + vdim)]
            wk[:, 2 * nope * j:2 * nope * (j + 1)] = jnp.concatenate([wa[:, :nope], wb[:, :nope]], axis=1)
            wv_t[2 * vdim * j:2 * vdim * (j + 1), :] = jnp.concatenate([wa.T[nope:], wb.T[nope:]], axis=0)

        @pl.loop(0, n_tile)
        def _(t):
            it = h * n_tile + t
            for k in range(2 * n_tile):
                if k % n_tile and plan[first_iter + k]:
                    @pl.when(it == k)
                    def _(k=k):
                        pump(plan[first_iter + k])
            @pl.when(it >= 3)
            def _():
                o_copy(it - 3).wait()

            @pl.when(it >= 2)
            def _():
                o_copy(it - 2).start()

            slot = lax.rem(it, 2)
            rows = pl.ds(pl.multiple_of(t * TILE, TILE), TILE)
            cq = cq_t[:, rows]
            for g in range(half_heads // chunk):
                w = wuq_t[g * chunk * hd:(g + 1) * chunk * hd, :]
                q = jnp.dot(w, cq, preferred_element_type=F32)
                for hh in range(chunk):
                    j, side = (g * chunk + hh) // 2, hh % 2
                    r0 = hh * hd
                    for p in range(2):
                        lanes = slice(seq * p, seq * (p + 1))
                        dst = slice(seq * side, seq * (side + 1))
                        qs[p, j, side * nope:(side + 1) * nope, dst] = q[r0:r0 + nope, lanes].astype(BF16)
                        lo = q[r0 + nope:r0 + nope + hr, lanes]
                        hi = q[r0 + nope + hr:r0 + hd, lanes]
                        qs[p, j, 2 * nope:2 * nope + hr, dst] = (lo * cos_q - hi * sin_q).astype(BF16)
                        qs[p, j, 2 * nope + hr:2 * nope + rope, dst] = (hi * cos_q + lo * sin_q).astype(BF16)
            lat = c_s[rows, :]
            ks[...] = jnp.dot(lat, wk[...], preferred_element_type=F32).astype(BF16)
            v = jnp.dot(wv_t[...], c_t[:, rows], preferred_element_type=F32).astype(BF16)
            for j in range(pairs):
                vs[slot, j, :2 * vdim, :] = v[2 * vdim * j:2 * vdim * (j + 1)]

            r_blk = [r_s[pl.ds(pl.multiple_of(t * TILE + p * seq, seq), seq), :] for p in range(2)]
            def scores(p, j):
                lhs = jnp.concatenate([ks[seq * p:seq * (p + 1), 2 * nope * j:2 * nope * (j + 1)], r_blk[p]], axis=1)
                s = jnp.dot(lhs, qs[p, j], preferred_element_type=F32)
                s = jnp.where(diff_s[...] >= 0, s, fill)
                s_buf[p, j] = s
                k = p * pairs + j
                top = jnp.max(s.reshape(groups, 8, 2 * seq), axis=0)
                pm[8 * k:8 * (k + 1), :] = top[:, :seq]
                pm[16 * pairs + 8 * k:16 * pairs + 8 * (k + 1), :] = top[:, seq:]

            for j in range(pairs):
                scores(0, j)
                values(1, j, 1 - slot, lax.rem(it + 2, 3))
            maxima(0)

            for j in range(pairs):
                scores(1, j)
                values(0, j, slot, lax.rem(it, 3))
            maxima(1)

    last = 2 * n_tile - 1
    o_copy(last - 2).wait()
    o_copy(last - 1).start()
    for j in range(pairs):
        values(1, j, last % 2, last % 3)
    o_copy(last).start()

    pump(plan[first_iter + 2 * n_tile])
    stage_out.wait()
    o_copy(last - 1).wait()
    o_copy(last).wait()
    c_out.wait()
    r_out.wait()
    for step in range(1, n_dev):
        gain_copy(step).wait_send()
    for it in items:
        for t in range(N_MSG):
            send(it, t).wait_send()


def out_kernel(o_ref, w_ref, x_ref, c_ref, r_ref, y_ref, c_out, r_out):
    acc = jnp.dot(o_ref[...], w_ref[...], preferred_element_type=F32)
    y_ref[...] = (x_ref[...].astype(F32) + acc).astype(BF16)
    c_out[...] = c_ref[...]
    seq = r_out.shape[2]
    for p in range(r_out.shape[0]):
        r_out[p] = r_ref[p * seq:(p + 1) * seq, :].T[:r_out.shape[1]]


def solution(mesh):
    batch_spec = P(('dp', 'fsdp'))
    row_spec = P('fsdp')
    mat_spec = P('fsdp', None)
    n_dev = mesh.shape['fsdp']
    assert n_dev == 8 and mesh.shape['dp'] % 2 == 0

    def local_block(tok, g_in, w_dq, g_q, w_uq, w_dkv, g_kv, w_ukv, w_out):
        n_p, seq, d_model = tok.shape
        n_tok = n_p * seq
        kv_rank, q_rank = g_kv.shape[0] * n_dev, g_q.shape[0] * n_dev
        rope = w_dkv.shape[1] - kv_rank
        nope_total = w_ukv.shape[1] - w_out.shape[0] * n_dev
        n_heads = (w_uq.shape[1] - nope_total) // rope
        nope = nope_total // n_heads
        vdim = w_out.shape[0] * n_dev // n_heads
        pairs = n_heads // 4
        hh = n_heads // 2
        x2 = tok.reshape(n_tok, d_model)
        gains = jnp.concatenate([g_in, g_q, g_kv]).astype(F32)
        gains = jnp.pad(gains, (0, -gains.shape[0] % 128))[None]
        cos, sin = rope_tables(seq, rope)
        cos_t, sin_t = jnp.asarray(cos.T), jnp.asarray(sin.T)
        reps = TILE // seq
        cos_n = jnp.asarray(np.tile(np.concatenate([cos, cos], 1), (reps, 1)))
        sin_n = jnp.asarray(np.tile(np.concatenate([-sin, sin], 1), (reps, 1)))
        dims = (n_dev, n_heads, nope, rope, vdim, d_model, q_rank, kv_rank, seq)
        n_items = len(SPLITS)
        any_ = pl.BlockSpec(memory_space=pl.ANY)
        vm = pl.BlockSpec(memory_space=pltpu.VMEM)
        o, wo_full, c_all, r_all = pl.pallas_call(
            functools.partial(gather_kernel, dims),
            out_shape=(
                jax.ShapeDtypeStruct((n_tok, n_heads * vdim), BF16),
                jax.ShapeDtypeStruct((n_heads * vdim, d_model), BF16),
                jax.ShapeDtypeStruct((n_tok, kv_rank), BF16),
                jax.ShapeDtypeStruct((n_tok, 128), BF16),
            ),
            in_specs=[any_] * 7 + [vm] * 4,
            out_specs=(any_,) * 4,
            scratch_shapes=[
                pltpu.VMEM((n_dev, 1, gains.shape[1]), F32),
                pltpu.VMEM((n_tok, d_model), BF16),
                pltpu.VMEM((d_model, q_rank), BF16),
                pltpu.VMEM((d_model, kv_rank + rope), BF16),
                pltpu.VMEM((n_tok, q_rank), F32),
                pltpu.VMEM((n_tok, kv_rank + rope), F32),
                pltpu.VMEM((q_rank, w_uq.shape[1]), BF16),
                pltpu.VMEM((w_uq.shape[1] // 2, q_rank), BF16),
                pltpu.VMEM((kv_rank, w_ukv.shape[1]), BF16),
                pltpu.VMEM((kv_rank, hh * nope), BF16),
                pltpu.VMEM((hh * vdim, kv_rank), BF16),
                pltpu.VMEM((q_rank, n_tok), BF16),
                pltpu.VMEM((n_tok, kv_rank), BF16),
                pltpu.VMEM((kv_rank, n_tok), BF16),
                pltpu.VMEM((n_tok, 128), BF16),
                pltpu.VMEM((2, pairs, 2 * nope + 128, 2 * seq), BF16),
                pltpu.VMEM((TILE, hh * nope), BF16),
                pltpu.VMEM((2, pairs, 2 * vdim + 16, TILE), BF16),
                pltpu.VMEM((3, TILE, hh * vdim), BF16),
                pltpu.VMEM(w_out.shape, BF16),
                pltpu.VMEM((seq, 2 * seq), jnp.int32),
                pltpu.VMEM((n_tok, 1), F32),
                pltpu.VMEM((8, d_model), F32),
                pltpu.VMEM((2, pairs, seq, 2 * seq), F32),
                pltpu.VMEM((2 * 2 * pairs * 8, seq), F32),
                pltpu.VMEM((2 * pairs, 2 * seq), F32),
                pltpu.SemaphoreType.DMA((n_items * N_MSG,)),
                pltpu.SemaphoreType.DMA((n_items * N_MSG,)),
                pltpu.SemaphoreType.DMA((10,)),
                pltpu.SemaphoreType.DMA((n_dev - 1,)),
                pltpu.SemaphoreType.DMA((n_dev - 1,)),
                pltpu.SemaphoreType.DMA((n_tok // TILE,)),
                pltpu.SemaphoreType.DMA((3,)),
                pltpu.SemaphoreType.DMA((2,)),
            ],
            compiler_params=pltpu.CompilerParams(
                collective_id=0, has_side_effects=True, vmem_limit_bytes=67_043_328
            ),
            name='gather_attend',
        )(x2, gains, w_dq, w_dkv, w_uq, w_ukv, w_out, cos_t, sin_t, cos_n, sin_n)

        bm, bn = 512, 1280
        n_m, n_n = n_tok // bm, d_model // bn
        once = lambda n, m: (jnp.where(n == 0, m, n_m - 1), 0)
        y, c_blk, r_blk = pl.pallas_call(
            out_kernel,
            grid=(n_n, n_m),
            in_specs=[
                pl.BlockSpec((bm, n_heads * vdim), lambda n, m: (m, 0)),
                pl.BlockSpec((n_heads * vdim, bn), lambda n, m: (0, n)),
                pl.BlockSpec((bm, bn), lambda n, m: (m, n)),
                pl.BlockSpec((bm, kv_rank), once),
                pl.BlockSpec((bm, 128), once),
            ],
            out_specs=[
                pl.BlockSpec((bm, bn), lambda n, m: (m, n)),
                pl.BlockSpec((bm, kv_rank), once),
                pl.BlockSpec((bm // seq, rope, seq), lambda n, m: (jnp.where(n == 0, m, n_m - 1), 0, 0)),
            ],
            out_shape=[
                jax.ShapeDtypeStruct((n_tok, d_model), BF16),
                jax.ShapeDtypeStruct((n_tok, kv_rank), BF16),
                jax.ShapeDtypeStruct((n_p, rope, seq), BF16),
            ],
            compiler_params=pltpu.CompilerParams(vmem_limit_bytes=60 * 1024 * 1024),
            name='project_out',
        )(o, wo_full, x2, c_all, r_all)
        return y.reshape(tok.shape), c_blk.reshape(n_p, seq, kv_rank), jnp.swapaxes(r_blk, 1, 2)

    return jax.shard_map(
        local_block,
        mesh=mesh,
        in_specs=(batch_spec, row_spec, mat_spec, row_spec, mat_spec, mat_spec, row_spec, mat_spec, mat_spec),
        out_specs=(batch_spec, batch_spec, batch_spec),
        check_vma=False,
    )
```

time: 216 us -> 147 us (0.68)
  Pallas kernels: 207 us -> 141 us
  local copies, waits for them, and re-layouts: 5.5 us -> 1.78 us
    pallas_call x1, Pallas kernels: 164 us -> 106 us  [local_block(): pl.pallas_call(functools.partial(gather_kernel, dims), out_shape=(jax.Sha...]
    pallas_call x1, Pallas kernels: 42.8 us -> 34.9 us  [local_block(): pl.pallas_call(out_kernel, grid=(n_n, n_m), in_specs=[pl.BlockSpec((bm, n...]
    unnamed x6 -> x1, local copies, waits for them, and re-layouts: 4.89 us -> 1.78 us
    dynamic_update_slice x3 -> x0, other arithmetic: 2.26 us -> none  [spread(): lax.dynamic_update_slice(jnp.zeros((total,), F32), g.astype(F32), (me * g...]
where the time goes in v2:
time: 147 us; the launch traced here: 145 us
  Pallas kernels  141 us (96%)
  local copies, waits for them, and re-layouts  1.78 us (1%)
    pallas_call x1, Pallas kernels, local_block(): pl.pallas_call(functools.partial(gather_kernel, dims), out_shape=(jax.Sha...  106 us
    pallas_call x1, Pallas kernels, local_block(): pl.pallas_call(out_kernel, grid=(n_n, n_m), in_specs=[pl.BlockSpec((bm, n...  34.9 us

profile of v2, /device:TPU:113, one launch (start us, length us, event | category | flops | bytes accessed | tf_op | source)
XLA Modules:
  0.0 144.9 jit_solution(9128617887378996864)
XLA Ops:
  0.6 1.4 fusion.5
  2.0 1.8 %copy.16.wdkv_l = bf16[320,288]{1,0:T(8,128)(2,1)} copy(bf16[320,288]{0,1:T(8,128)(2,1)} %param.18) | data formatting | bytes 368640 | tf_op args[5]
  3.8 106.3 %gather_attend.1 = (bf16[2048,2560]{1,0:T(8,128)(2,1)}, bf16[2560,2560]{1,0:T(8,128)(2,1)}, bf16[2048,256]{1,0:T(8,128)(2,1)}, bf16[2048,128]{1,0:T(8,128)(2,1)}) custom-call(bf16[2048,2560]{1,0:T(8,128)(2,1)} %bitcast.5, f32[1,512]{1,0:T(1,128)} %bitcast.7, bf16[320,768]{1,0:T(8,128)(2,1)} %wdq_l.1, bf16[320,288]{1,0:T(8,128)(2,1)} %copy.16.wdkv_l, ...), custom_call_target="tpu_custom_call" | custom-call | tf_op jit(solution)/shard_map/gather_attend/pallas_call | solution.py:536
  110.0 34.9 %project_out.1 = (bf16[2048,2560]{1,0:T(8,128)(2,1)}, bf16[2048,256]{1,0:T(8,128)(2,1)}, bf16[16,32,128]{2,1,0:T(8,128)(2,1)}) custom-call(bf16[2048,2560]{1,0:T(8,128)(2,1)} %get-tuple-element.10.o_ref, bf16[2560,2560]{1,0:T(8,128)(2,1)} %get-tuple-element.11.w_ref, bf16[2048,2560]{1,0:T(8,128)(2,1)} %bitcast.6, bf16[2048,256]{1,0:T(8,128)(2,1)} %get-tuple-element.12.c_ref, ...), custom_call_target="tpu_custom_call" | custom-call | tf_op jit(solution)/shard_map/project_out/pallas_call | solution.py:591
